TPU v7x, 8 devices: a whole 2x2x1 slice. The times are simulated.
8 devices in a mesh: dp: 1 (over z), sx: 2 (over y), sy: 4 (over x, core).
Axes of the slice: x: 2, y: 2, z: 1, core: 2. Of those that a mesh axis runs over, the one named last changes fastest.
Arguments:
- act_in: bfloat16 [12, 2048, 16, 256], P('dp', 'sy', 'sx')
- norm_first: bfloat16 [2, 256], replicated
- w_first: bfloat16 [3, 3, 256, 128], replicated
- w_short: bfloat16 [256, 128], replicated
- norm_rest: bfloat16 [6, 2, 128], replicated
- w_rest: bfloat16 [5, 3, 3, 128, 128], replicated
- bias_rest: bfloat16 [7, 128], replicated
- w_out: bfloat16 [3, 3, 128, 3], replicated
- bias_out: bfloat16 [3], replicated
Outputs:
- output: float32 [12, 2048, 16, 3], P('dp', 'sy', 'sx')
All inputs are finite; a program needn't handle non-finite values.
Results may differ from a plain program's by a relative error of at most 0.00841722.
Values are sent between devices in bfloat16 or wider.
A program may use at most 1 GiB of HBM per device.

v0:
```python
import jax
import jax.numpy as jnp
from jax import lax
from jax.sharding import PartitionSpec as P

GROUPS = 32
GN_EPS = 1e-6


def solution(mesh):
    rows_n = mesh.shape["sy"]
    cols_n = mesh.shape["sx"]
    to_below = [(position, position + 1) for position in range(rows_n - 1)]
    to_above = [(position + 1, position) for position in range(rows_n - 1)]
    to_right = [(position, position + 1) for position in range(cols_n - 1)]
    to_left = [(position + 1, position) for position in range(cols_n - 1)]
    tile_spec = P("dp", "sy", "sx", None)
    replicated = P()

    def add_border(act_map):
        top_row = lax.ppermute(act_map[:, -1:], "sy", to_below)
        bottom_row = lax.ppermute(act_map[:, :1], "sy", to_above)
        tall = jnp.concatenate([top_row, act_map, bottom_row], axis=1)
        left_col = lax.ppermute(tall[:, :, -1:], "sx", to_right)
        right_col = lax.ppermute(tall[:, :, :1], "sx", to_left)
        return jnp.concatenate([left_col, tall, right_col], axis=2)

    def conv_tile(act_map, kernel):
        return lax.conv_general_dilated(add_border(act_map), kernel, (1, 1), ((0, 0), (0, 0)), dimension_numbers=("NHWC", "HWIO", "NHWC"), preferred_element_type=jnp.float32)

    def group_norm_act(act_map, norm_pair):
        samples = act_map.shape[0]
        per_group = act_map.shape[3] // GROUPS
        group_count = act_map.shape[1] * rows_n * act_map.shape[2] * cols_n * per_group
        sum_one = jnp.sum(act_map, axis=(1, 2), dtype=jnp.float32).reshape(samples, GROUPS, per_group).sum(axis=2)
        sum_two = jnp.sum(jnp.square(act_map.astype(jnp.float32)), axis=(1, 2)).reshape(samples, GROUPS, per_group).sum(axis=2)
        totals = lax.psum(jnp.stack([sum_one, sum_two], axis=-1), ("sy", "sx"))
        group_mean = totals[:, :, 0] / group_count
        inv_std = lax.rsqrt(totals[:, :, 1] / group_count - group_mean * group_mean + GN_EPS)
        chan_scale = jnp.repeat(inv_std, per_group, axis=1) * norm_pair[0].astype(jnp.float32)
        chan_shift = norm_pair[1].astype(jnp.float32) - jnp.repeat(group_mean, per_group, axis=1) * chan_scale
        return jax.nn.silu(act_map.astype(jnp.float32) * chan_scale[:, None, None, :] + chan_shift[:, None, None, :]).astype(jnp.bfloat16)

    def local_decode(act_in, norm_first, w_first, w_short, norm_rest, w_rest, bias_rest, w_out, bias_out):
        bias_rows = bias_rest.astype(jnp.float32)
        mid_act = (conv_tile(group_norm_act(act_in, norm_first), w_first) + bias_rows[0]).astype(jnp.bfloat16)
        skip_path = jnp.einsum("nhwc,cd->nhwd", act_in, w_short, preferred_element_type=jnp.float32) + bias_rows[6]
        hidden = (conv_tile(group_norm_act(mid_act, norm_rest[0]), w_rest[0]) + bias_rows[1] + skip_path).astype(jnp.bfloat16)
        for res_index in range(1, 3):
            first_at = 2 * res_index - 1
            mid_act = (conv_tile(group_norm_act(hidden, norm_rest[first_at]), w_rest[first_at]) + bias_rows[first_at + 1]).astype(jnp.bfloat16)
            hidden = (conv_tile(group_norm_act(mid_act, norm_rest[first_at + 1]), w_rest[first_at + 1]) + bias_rows[first_at + 2] + hidden.astype(jnp.float32)).astype(jnp.bfloat16)
        return conv_tile(group_norm_act(hidden, norm_rest[5]), w_out) + bias_out.astype(jnp.float32)

    return jax.shard_map(local_decode, mesh=mesh, in_specs=(tile_spec, replicated, replicated, replicated, replicated, replicated, replicated, replicated, replicated), out_specs=tile_spec, check_vma=False)
```

profile of v0, /device:TPU:0, one launch (start us, length us, event | category | flops | bytes accessed | tf_op | source)
XLA Modules:
  0.0 1280.5 jit_solution(8018396413084928872)
XLA Ops:
  0.0 45.1 %convert_reduce_fusion = (f32[12,256]{1,0:T(8,128)S(1)}, f32[12,256]{1,0:T(8,128)S(1)}) fusion(bf16[12,512,8,256]{3,2,1,0:T(8,128)(2,1)} %param.9), kind=kLoop, calls=%fused_computation.2 | loop fusion | flops 50325504 | bytes 25190400 | tf_op jit(solution)/shard_map/reduce_sum | solution.py:35
  45.6 25.2 %psum.49 = f32[12,32,2]{1,0,2:T(8,128)S(1)} all-reduce(f32[12,32,2]{1,0,2:T(8,128)S(1)} %pad_maximum_fusion.21), channel_id=1, replica_groups=mesh['dp'=1,'sx'=2,'sy'=4] {'sy','sx'}, use_global_device_ids=true, to_apply=%region_4.0 | all-reduce | flops 768 | bytes 6144 | tf_op jit(solution)/shard_map/psum | solution.py:37
  71.4 48.8 %fusion.7 = bf16[12,512,8,256]{3,0,2,1:T(8,128)(2,1)} fusion(bf16[12,512,8,256]{3,2,1,0:T(8,128)(2,1)} %param.9, f32[12,256]{1,0:T(8,128)S(1)} %get-tuple-element.31, f32[12,256]{1,0:T(8,128)S(1)} %get-tuple-element.32), kind=kLoop, calls=%fused_computation.10 | loop fusion | flops 100663296 | bytes 50356224 | tf_op jit(solution)/shard_map/convert_element_type | solution.py:42
  140.4 63.4 %collective-permute-done.2 = bf16[12,514,1,256]{3,1,2,0:T(8,128)(2,1)S(1)} collective-permute-done((bf16[12,514,1,256]{3,1,2,0:T(8,128)(2,1)S(1)}, bf16[12,514,1,256]{3,1,2,0:T(8,128)(2,1)S(1)}, u32[]{:S(2)}, u32[]{:S(2)}) %collective-permute-start.2) | collective-permute-done | bytes 3158048 | tf_op jit(solution)/shard_map/ppermute | solution.py:24
  204.5 5.3 collective-permute-done.3
  210.6 87.1 %convert_reduce_fusion.6 = (f32[12,128]{1,0:T(8,128)S(1)}, f32[12,128]{1,0:T(8,128)S(1)}, bf16[12,512,8,128]{3,0,2,1:T(8,128)(2,1)}) fusion(f32[128]{0:T(128)S(1)} %get-tuple-element.67, bf16[3,3,256,128]{3,2,1,0:T(8,128)(2,1)S(1)} %copy-done, bf16[12,514,1,256]{3,0,2,1:T(8,128)(2,1)S(1)} %copy.345, bf16[12,1,8,256]{3,0,2,1:T(8,128)(2,1)S(1)} %collective-permute-done.1, ...), kind=kOutput, calls=%fused_computation.30 | convolution fusion | flops 29091934208 | bytes 44765696 | tf_op jit(solution)/shard_map/conv_general_dilated | solution.py:29
  298.3 22.7 %psum.50 = f32[12,32,2]{1,0,2:T(8,128)S(1)} all-reduce(f32[12,32,2]{1,0,2:T(8,128)S(1)} %pad_maximum_fusion.22), channel_id=1, replica_groups=mesh['dp'=1,'sx'=2,'sy'=4] {'sy','sx'}, use_global_device_ids=true, to_apply=%region_9.10 | all-reduce | flops 768 | bytes 6144 | tf_op jit(solution)/shard_map/psum | solution.py:37
  321.4 12.8 fusion.25
  348.3 20.4 %fusion.155 = f32[12,512,8,128]{3,2,1,0:T(8,128)} fusion(bf16[12,512,8,256]{3,2,1,0:T(8,128)(2,1)} %param.9, bf16[256,128]{1,0:T(8,128)(2,1)S(1)} %copy-done.4), kind=kOutput, calls=%fused_computation.189 | convolution fusion | flops 3221225472 | bytes 50397184 | tf_op jit(solution)/shard_map/nhwc,cd->nhwd/dot_general | solution.py:47
  368.7 11.4 collective-permute-done.6
  387.1 59.8 %convert_reduce_fusion.2 = (f32[12,128]{1,0:T(8,128)S(1)}, f32[12,128]{1,0:T(8,128)S(1)}, bf16[12,512,8,128]{3,0,2,1:T(8,128)(2,1)}) fusion(f32[128]{0:T(128)S(1)} %get-tuple-element.65, f32[12,512,8,128]{3,2,1,0:T(8,128)} %fusion.155, f32[128]{0:T(128)S(1)} %get-tuple-element.66, bf16[12,514,1,128]{3,0,2,1:T(8,128)(2,1)S(1)} %copy.357, ...), kind=kOutput, calls=%fused_computation.18 | convolution fusion | flops 14577422336 | bytes 53847040 | tf_op jit(solution)/shard_map/conv_general_dilated | solution.py:29
  447.4 22.5 %psum.51 = f32[12,32,2]{1,0,2:T(8,128)S(1)} all-reduce(f32[12,32,2]{1,0,2:T(8,128)S(1)} %pad_maximum_fusion.23), channel_id=1, replica_groups=mesh['dp'=1,'sx'=2,'sy'=4] {'sy','sx'}, use_global_device_ids=true, to_apply=%region_14.15 | all-reduce | flops 768 | bytes 6144 | tf_op jit(solution)/shard_map/psum | solution.py:37
  470.4 12.8 fusion.57
  497.1 31.8 %collective-permute-done.10 = bf16[12,514,1,128]{3,1,2,0:T(8,128)(2,1)S(1)} collective-permute-done((bf16[12,514,1,128]{3,1,2,0:T(8,128)(2,1)S(1)}, bf16[12,514,1,128]{3,1,2,0:T(8,128)(2,1)S(1)}, u32[]{:S(2)}, u32[]{:S(2)}) %collective-permute-start.10) | collective-permute-done | bytes 1579040 | tf_op jit(solution)/shard_map/ppermute | solution.py:24
  534.5 42.3 %convert_reduce_fusion.5 = (f32[12,128]{1,0:T(8,128)S(1)}, f32[12,128]{1,0:T(8,128)S(1)}, bf16[12,512,8,128]{3,0,2,1:T(8,128)(2,1)}) fusion(f32[128]{0:T(128)S(1)} %copy-done.21, bf16[5,3,3,128,128]{4,3,2,1,0:T(8,128)(2,1)S(1)} %copy-done.3, bf16[12,514,1,128]{3,0,2,1:T(8,128)(2,1)S(1)} %copy.371, bf16[12,1,8,128]{3,0,2,1:T(8,128)(2,1)S(1)} %collective-permute-done.9, ...), kind=kOutput, calls=%fused_computation.27 | convolution fusion | flops 14564839424 | bytes 33944064 | tf_op jit(solution)/shard_map/conv_general_dilated | solution.py:29
  577.2 22.7 %psum.52 = f32[12,32,2]{1,0,2:T(8,128)S(1)} all-reduce(f32[12,32,2]{1,0,2:T(8,128)S(1)} %pad_maximum_fusion.24), channel_id=1, replica_groups=mesh['dp'=1,'sx'=2,'sy'=4] {'sy','sx'}, use_global_device_ids=true, to_apply=%region_19.20 | all-reduce | flops 768 | bytes 6144 | tf_op jit(solution)/shard_map/psum | solution.py:37
  600.4 12.8 fusion.33
  626.9 31.8 %collective-permute-done.14 = bf16[12,514,1,128]{3,1,2,0:T(8,128)(2,1)S(1)} collective-permute-done((bf16[12,514,1,128]{3,1,2,0:T(8,128)(2,1)S(1)}, bf16[12,514,1,128]{3,1,2,0:T(8,128)(2,1)S(1)}, u32[]{:S(2)}, u32[]{:S(2)}) %collective-permute-start.14) | collective-permute-done | bytes 1579040 | tf_op jit(solution)/shard_map/ppermute | solution.py:24
  664.3 46.5 %convert_reduce_fusion.1 = (f32[12,128]{1,0:T(8,128)S(1)}, f32[12,128]{1,0:T(8,128)S(1)}, bf16[12,512,8,128]{3,0,2,1:T(8,128)(2,1)}) fusion(bf16[12,512,8,128]{3,0,2,1:T(8,128)(2,1)} %get-tuple-element.83, f32[128]{0:T(128)S(1)} %copy-done.20, bf16[12,514,1,128]{3,0,2,1:T(8,128)(2,1)S(1)} %copy.383, ...), kind=kOutput, calls=%fused_computation.14 | convolution fusion | flops 14577422336 | bytes 41263616 | tf_op jit(solution)/shard_map/conv_general_dilated | solution.py:29
  711.3 22.3 %psum.53 = f32[12,32,2]{1,0,2:T(8,128)S(1)} all-reduce(f32[12,32,2]{1,0,2:T(8,128)S(1)} %pad_maximum_fusion.25), channel_id=1, replica_groups=mesh['dp'=1,'sx'=2,'sy'=4] {'sy','sx'}, use_global_device_ids=true, to_apply=%region_24.25 | all-reduce | flops 768 | bytes 6144 | tf_op jit(solution)/shard_map/psum | solution.py:37
  734.1 12.8 fusion.66
  760.8 31.6 %collective-permute-done.18 = bf16[12,514,1,128]{3,1,2,0:T(8,128)(2,1)S(1)} collective-permute-done((bf16[12,514,1,128]{3,1,2,0:T(8,128)(2,1)S(1)}, bf16[12,514,1,128]{3,1,2,0:T(8,128)(2,1)S(1)}, u32[]{:S(2)}, u32[]{:S(2)}) %collective-permute-start.18) | collective-permute-done | bytes 1579040 | tf_op jit(solution)/shard_map/ppermute | solution.py:24
  798.2 42.2 %convert_reduce_fusion.4 = (f32[12,128]{1,0:T(8,128)S(1)}, f32[12,128]{1,0:T(8,128)S(1)}, bf16[12,512,8,128]{3,0,2,1:T(8,128)(2,1)}) fusion(f32[128]{0:T(128)S(1)} %copy-done.19, bf16[5,3,3,128,128]{4,3,2,1,0:T(8,128)(2,1)S(1)} %copy-done.3, bf16[12,514,1,128]{3,0,2,1:T(8,128)(2,1)S(1)} %copy.395, bf16[12,1,8,128]{3,0,2,1:T(8,128)(2,1)S(1)} %collective-permute-done.17, ...), kind=kOutput, calls=%fused_computation.24 | convolution fusion | flops 14564839424 | bytes 33944064 | tf_op jit(solution)/shard_map/conv_general_dilated | solution.py:29
  840.9 22.3 %psum.54 = f32[12,32,2]{1,0,2:T(8,128)S(1)} all-reduce(f32[12,32,2]{1,0,2:T(8,128)S(1)} %pad_maximum_fusion.26), channel_id=1, replica_groups=mesh['dp'=1,'sx'=2,'sy'=4] {'sy','sx'}, use_global_device_ids=true, to_apply=%region_29.30 | all-reduce | flops 768 | bytes 6144 | tf_op jit(solution)/shard_map/psum | solution.py:37
  863.7 12.8 fusion.41
  890.5 31.4 %collective-permute-done.22 = bf16[12,514,1,128]{3,1,2,0:T(8,128)(2,1)S(1)} collective-permute-done((bf16[12,514,1,128]{3,1,2,0:T(8,128)(2,1)S(1)}, bf16[12,514,1,128]{3,1,2,0:T(8,128)(2,1)S(1)}, u32[]{:S(2)}, u32[]{:S(2)}) %collective-permute-start.22) | collective-permute-done | bytes 1579040 | tf_op jit(solution)/shard_map/ppermute | solution.py:24
  927.6 46.6 %convert_reduce_fusion.3 = (f32[12,128]{1,0:T(8,128)S(1)}, f32[12,128]{1,0:T(8,128)S(1)}, bf16[12,512,8,128]{3,0,2,1:T(8,128)(2,1)}) fusion(bf16[12,512,8,128]{3,0,2,1:T(8,128)(2,1)} %get-tuple-element.85, f32[128]{0:T(128)S(1)} %copy-done.18, bf16[12,514,1,128]{3,0,2,1:T(8,128)(2,1)S(1)} %copy.407, ...), kind=kOutput, calls=%fused_computation.21 | convolution fusion | flops 14577422336 | bytes 41263616 | tf_op jit(solution)/shard_map/conv_general_dilated | solution.py:29
  974.6 22.4 %psum.55 = f32[12,32,2]{1,0,2:T(8,128)S(1)} all-reduce(f32[12,32,2]{1,0,2:T(8,128)S(1)} %pad_maximum_fusion.27), channel_id=1, replica_groups=mesh['dp'=1,'sx'=2,'sy'=4] {'sy','sx'}, use_global_device_ids=true, to_apply=%region_34.35 | all-reduce | flops 768 | bytes 6144 | tf_op jit(solution)/shard_map/psum | solution.py:37
  997.4 12.8 fusion.49
  1024.0 31.8 %collective-permute-done.26 = bf16[12,514,1,128]{3,1,2,0:T(8,128)(2,1)S(1)} collective-permute-done((bf16[12,514,1,128]{3,1,2,0:T(8,128)(2,1)S(1)}, bf16[12,514,1,128]{3,1,2,0:T(8,128)(2,1)S(1)}, u32[]{:S(2)}, u32[]{:S(2)}) %collective-permute-start.26) | collective-permute-done | bytes 1579040 | tf_op jit(solution)/shard_map/ppermute | solution.py:24
  1061.3 212.4 %fusion.142 = f32[12,512,8,3]{0,3,2,1:T(4,128)} fusion(bf16[3,3,128,3]{2,3,1,0:T(4,128)(2,1)S(1)} %copy-done.22, bf16[12,514,1,128]{3,0,2,1:T(8,128)(2,1)S(1)} %copy.419, bf16[12,1,8,128]{3,0,2,1:T(8,128)(2,1)S(1)} %collective-permute-done.25, bf16[12,512,8,128]{3,0,2,1:T(8,128)(2,1)S(1)} %fusion.49, ...), kind=kOutput, calls=%fused_computation.157 | convolution fusion | flops 371466240 | bytes 16386828 | tf_op jit(solution)/shard_map/conv_general_dilated | solution.py:29
  1273.7 6.6 copy.420
  (254 shorter events, 145.8 us)
Async XLA Ops:
  0.0 210.6 %copy-start = (bf16[3,3,256,128]{3,2,1,0:T(8,128)(2,1)S(1)}, bf16[3,3,256,128]{3,2,1,0:T(8,128)(2,1)}, u32[]{:S(2)}) copy-start(bf16[3,3,256,128]{3,2,1,0:T(8,128)(2,1)} %param.11) | copy-start | bytes 1769476
  121.1 2.6 collective-permute-start
  122.4 5.7 collective-permute-start.1
  133.7 70.0 %collective-permute-start.2 = (bf16[12,514,1,256]{3,1,2,0:T(8,128)(2,1)S(1)}, bf16[12,514,1,256]{3,1,2,0:T(8,128)(2,1)S(1)}, u32[]{:S(2)}, u32[]{:S(2)}) collective-permute-start(bf16[12,514,1,256]{3,1,2,0:T(8,128)(2,1)S(1)} %copy.342), channel_id=1, source_target_pairs={{0,4},{1,5},{2,6},{3,7}} | collective-permute-start | bytes 9474056 | tf_op jit(solution)/shard_map/ppermute | solution.py:24
  137.6 72.2 %collective-permute-start.3 = (bf16[12,514,1,256]{3,1,2,0:T(8,128)(2,1)S(1)}, bf16[12,514,1,256]{3,1,2,0:T(8,128)(2,1)S(1)}, u32[]{:S(2)}, u32[]{:S(2)}) collective-permute-start(bf16[12,514,1,256]{3,1,2,0:T(8,128)(2,1)S(1)} %copy.343), channel_id=1, source_target_pairs={{4,0},{5,1},{6,2},{7,3}} | collective-permute-start | bytes 9474056 | tf_op jit(solution)/shard_map/ppermute | solution.py:25
  334.2 4.0 collective-permute-start.4
  335.6 5.6 collective-permute-start.5
  343.0 37.1 %collective-permute-start.6 = (bf16[12,514,1,128]{3,1,2,0:T(8,128)(2,1)S(1)}, bf16[12,514,1,128]{3,1,2,0:T(8,128)(2,1)S(1)}, u32[]{:S(2)}, u32[]{:S(2)}) collective-permute-start(bf16[12,514,1,128]{3,1,2,0:T(8,128)(2,1)S(1)} %copy.354), channel_id=1, source_target_pairs={{0,4},{1,5},{2,6},{3,7}} | collective-permute-start | bytes 4737032 | tf_op jit(solution)/shard_map/ppermute | solution.py:24
  347.0 38.3 %collective-permute-start.7 = (bf16[12,514,1,128]{3,1,2,0:T(8,128)(2,1)S(1)}, bf16[12,514,1,128]{3,1,2,0:T(8,128)(2,1)}, u32[]{:S(2)}, u32[]{:S(2)}) collective-permute-start(bf16[12,514,1,128]{3,1,2,0:T(8,128)(2,1)S(1)} %copy.355), channel_id=1, source_target_pairs={{4,0},{5,1},{6,2},{7,3}} | collective-permute-start | bytes 4737032 | tf_op jit(solution)/shard_map/ppermute | solution.py:25
  387.1 83.2 %copy-start.15 = (f32[128]{0:T(128)S(1)}, f32[128]{0:T(128)}, u32[]{:S(2)}) copy-start(f32[128]{0:T(128)} %get-tuple-element.75) | copy-start | bytes 1540
  387.1 83.2 %copy-start.16 = (f32[128]{0:T(128)S(1)}, f32[128]{0:T(128)}, u32[]{:S(2)}) copy-start(f32[128]{0:T(128)} %get-tuple-element.76) | copy-start | bytes 1540
  483.2 2.8 collective-permute-start.8
  484.5 5.7 collective-permute-start.9
  492.0 36.8 %collective-permute-start.10 = (bf16[12,514,1,128]{3,1,2,0:T(8,128)(2,1)S(1)}, bf16[12,514,1,128]{3,1,2,0:T(8,128)(2,1)S(1)}, u32[]{:S(2)}, u32[]{:S(2)}) collective-permute-start(bf16[12,514,1,128]{3,1,2,0:T(8,128)(2,1)S(1)} %copy.368), channel_id=1, source_target_pairs={{0,4},{1,5},{2,6},{3,7}} | collective-permute-start | bytes 4737032 | tf_op jit(solution)/shard_map/ppermute | solution.py:24
  495.8 38.3 %collective-permute-start.11 = (bf16[12,514,1,128]{3,1,2,0:T(8,128)(2,1)S(1)}, bf16[12,514,1,128]{3,1,2,0:T(8,128)(2,1)S(1)}, u32[]{:S(2)}, u32[]{:S(2)}) collective-permute-start(bf16[12,514,1,128]{3,1,2,0:T(8,128)(2,1)S(1)} %copy.369), channel_id=1, source_target_pairs={{4,0},{5,1},{6,2},{7,3}} | collective-permute-start | bytes 4737032 | tf_op jit(solution)/shard_map/ppermute | solution.py:25
  613.1 2.6 collective-permute-start.12
  614.5 5.6 collective-permute-start.13
  621.9 36.8 %collective-permute-start.14 = (bf16[12,514,1,128]{3,1,2,0:T(8,128)(2,1)S(1)}, bf16[12,514,1,128]{3,1,2,0:T(8,128)(2,1)S(1)}, u32[]{:S(2)}, u32[]{:S(2)}) collective-permute-start(bf16[12,514,1,128]{3,1,2,0:T(8,128)(2,1)S(1)} %copy.380), channel_id=1, source_target_pairs={{0,4},{1,5},{2,6},{3,7}} | collective-permute-start | bytes 4737032 | tf_op jit(solution)/shard_map/ppermute | solution.py:24
  625.6 38.3 %collective-permute-start.15 = (bf16[12,514,1,128]{3,1,2,0:T(8,128)(2,1)S(1)}, bf16[12,514,1,128]{3,1,2,0:T(8,128)(2,1)S(1)}, u32[]{:S(2)}, u32[]{:S(2)}) collective-permute-start(bf16[12,514,1,128]{3,1,2,0:T(8,128)(2,1)S(1)} %copy.381), channel_id=1, source_target_pairs={{4,0},{5,1},{6,2},{7,3}} | collective-permute-start | bytes 4737032 | tf_op jit(solution)/shard_map/ppermute | solution.py:25
  746.9 2.6 collective-permute-start.16
  748.2 5.6 collective-permute-start.17
  755.6 36.8 %collective-permute-start.18 = (bf16[12,514,1,128]{3,1,2,0:T(8,128)(2,1)S(1)}, bf16[12,514,1,128]{3,1,2,0:T(8,128)(2,1)S(1)}, u32[]{:S(2)}, u32[]{:S(2)}) collective-permute-start(bf16[12,514,1,128]{3,1,2,0:T(8,128)(2,1)S(1)} %copy.392), channel_id=1, source_target_pairs={{0,4},{1,5},{2,6},{3,7}} | collective-permute-start | bytes 4737032 | tf_op jit(solution)/shard_map/ppermute | solution.py:24
  759.5 38.3 %collective-permute-start.19 = (bf16[12,514,1,128]{3,1,2,0:T(8,128)(2,1)S(1)}, bf16[12,514,1,128]{3,1,2,0:T(8,128)(2,1)S(1)}, u32[]{:S(2)}, u32[]{:S(2)}) collective-permute-start(bf16[12,514,1,128]{3,1,2,0:T(8,128)(2,1)S(1)} %copy.393), channel_id=1, source_target_pairs={{4,0},{5,1},{6,2},{7,3}} | collective-permute-start | bytes 4737032 | tf_op jit(solution)/shard_map/ppermute | solution.py:25
  876.5 2.6 collective-permute-start.20
  877.8 5.6 collective-permute-start.21
  885.2 36.8 %collective-permute-start.22 = (bf16[12,514,1,128]{3,1,2,0:T(8,128)(2,1)S(1)}, bf16[12,514,1,128]{3,1,2,0:T(8,128)(2,1)S(1)}, u32[]{:S(2)}, u32[]{:S(2)}) collective-permute-start(bf16[12,514,1,128]{3,1,2,0:T(8,128)(2,1)S(1)} %copy.404), channel_id=1, source_target_pairs={{0,4},{1,5},{2,6},{3,7}} | collective-permute-start | bytes 4737032 | tf_op jit(solution)/shard_map/ppermute | solution.py:24
  888.9 38.3 %collective-permute-start.23 = (bf16[12,514,1,128]{3,1,2,0:T(8,128)(2,1)S(1)}, bf16[12,514,1,128]{3,1,2,0:T(8,128)(2,1)S(1)}, u32[]{:S(2)}, u32[]{:S(2)}) collective-permute-start(bf16[12,514,1,128]{3,1,2,0:T(8,128)(2,1)S(1)} %copy.405), channel_id=1, source_target_pairs={{4,0},{5,1},{6,2},{7,3}} | collective-permute-start | bytes 4737032 | tf_op jit(solution)/shard_map/ppermute | solution.py:25
  1010.2 2.6 collective-permute-start.24
  1011.5 5.6 collective-permute-start.25
  1018.9 36.8 %collective-permute-start.26 = (bf16[12,514,1,128]{3,1,2,0:T(8,128)(2,1)S(1)}, bf16[12,514,1,128]{3,1,2,0:T(8,128)(2,1)S(1)}, u32[]{:S(2)}, u32[]{:S(2)}) collective-permute-start(bf16[12,514,1,128]{3,1,2,0:T(8,128)(2,1)S(1)} %copy.416), channel_id=1, source_target_pairs={{0,4},{1,5},{2,6},{3,7}} | collective-permute-start | bytes 4737032 | tf_op jit(solution)/shard_map/ppermute | solution.py:24
  1022.7 38.3 %collective-permute-start.27 = (bf16[12,514,1,128]{3,1,2,0:T(8,128)(2,1)S(1)}, bf16[12,514,1,128]{3,1,2,0:T(8,128)(2,1)S(1)}, u32[]{:S(2)}, u32[]{:S(2)}) collective-permute-start(bf16[12,514,1,128]{3,1,2,0:T(8,128)(2,1)S(1)} %copy.417), channel_id=1, source_target_pairs={{4,0},{5,1},{6,2},{7,3}} | collective-permute-start | bytes 4737032 | tf_op jit(solution)/shard_map/ppermute | solution.py:25
  1061.3 219.0 %copy-start.1 = (bf16[3,3,256,128]{3,2,1,0:T(8,128)(2,1)S(1)}, bf16[3,3,256,128]{3,2,1,0:T(8,128)(2,1)}, u32[]{:S(2)}) copy-start(bf16[3,3,256,128]{3,2,1,0:T(8,128)(2,1)} %param.11) | copy-start | bytes 1769476
  (20 other events, 980.9 us)
where the time goes:
time: 1290 us; the launch traced here: 1280 us
  matrix products  557 us (43%)
  waiting for transfers between devices  297 us (23%)
  other arithmetic  185 us (14%)
  blocking collectives  160 us (12%)
  starting transfers between devices  50.7 us (4%)
  local copies, waits for them, and re-layouts  28.8 us (2%)
    conv_general_dilated x7, matrix products, conv_tile(): lax.conv_general_dilated(add_border(act_map), kernel, (1, 1), ((0, 0), (0...  537 us
    ppermute x7, waiting for transfers between devices, add_border(): left_col = lax.ppermute(tall[:, :, -1:], 'sx', to_right)  233 us
    psum x7, blocking collectives, group_norm_act(): totals = lax.psum(jnp.stack([sum_one, sum_two], axis=-1), ('sy', 'sx'))  160 us
    convert_element_type x7, other arithmetic, group_norm_act(): jax.nn.silu(act_map.astype(jnp.float32) * chan_scale[:, None, None, :] +...  125 us
    reduce_sum x8, other arithmetic, group_norm_act(): jnp.sum(act_map, axis=(1, 2), dtype=jnp.float32)  45.5 us
    ppermute x7, waiting for transfers between devices, add_border(): right_col = lax.ppermute(tall[:, :, :1], 'sx', to_left)  34.7 us
    ppermute x7, waiting for transfers between devices, add_border(): bottom_row = lax.ppermute(act_map[:, :1], 'sy', to_above)  28.9 us
  transfers between devices with their start and end apart: 28, of which 21 were waited for; matrix products, arithmetic and copies ran while one was open for 2% of the time, Pallas kernels for 0%

commit v1 on v0

v1 whole, which is shorter than its diff:
```python
import functools

import jax
import jax.numpy as jnp
from jax import lax
from jax.experimental import pallas as pl
from jax.experimental.pallas import tpu as pltpu
from jax.sharding import PartitionSpec as P

GROUPS = 32
GN_EPS = 1e-6
LANES = 128
SEGS = 16
MESH = pl.DeviceIdType.MESH
F32 = jnp.float32
BF16 = jnp.bfloat16


def decode_kernel(cfg, a_hbm, nf_ref, wf_hbm, ws_hbm, nr_ref, wr_hbm, br_ref, wo_ref, bo_ref, out_ref,
                  wide, thin, act, w_one, w_two, w_mid, halo_even, halo_odd, land, shuffle, bias_f,
                  row_send, row_recv, cor_send, cor_recv, stat,
                  land_sem, w_sem, col_ss, col_rs, row_ss, row_rs, cor_ss, cor_rs, stat_ss, stat_rs):
    samples, segrows, cols, n_sx, n_sy = cfg
    devices = n_sx * n_sy
    px = segrows * SEGS
    sx = lax.axis_index("sx")
    sy = lax.axis_index("sy")
    me = sx * n_sy + sy
    edge = (cols - 1) * (1 - sx)
    pixels = segrows * SEGS * cols * devices

    barrier = pltpu.get_barrier_semaphore()
    peers = []
    for k in range(1, devices):
        peers.append({"sx": lax.rem(sx + k // n_sy, n_sx), "sy": lax.rem(sy + k % n_sy, n_sy)})
    for peer in peers:
        pl.semaphore_signal(barrier, inc=1, device_id=peer, device_id_type=MESH)

    def land_copy(i, slot):
        return pltpu.make_async_copy(a_hbm.at[i], land.at[slot], land_sem.at[slot])

    land_copy(0, 0).start()

    weight_copies = []
    for e in range(2):
        lanes = pl.ds(e * LANES, LANES)
        for dr in range(3):
            weight_copies.append((wf_hbm.at[dr], w_one.at[dr, pl.ds(e, 3), :, lanes]))
            weight_copies.append((wr_hbm.at[0, dr], w_two.at[dr, pl.ds(e, 3), :, lanes]))
            for layer in range(4):
                weight_copies.append((wr_hbm.at[layer + 1, dr], w_mid.at[layer, dr, pl.ds(e, 3), :, lanes]))
        for half in range(2):
            weight_copies.append((ws_hbm.at[pl.ds(half * LANES, LANES)], w_two.at[3, 2 * e + half, :, lanes]))
    weight_copies = [pltpu.make_async_copy(src, dst, w_sem.at[n]) for n, (src, dst) in enumerate(weight_copies)]
    for copy in weight_copies:
        copy.start()
    zero_one = jnp.zeros((2 * LANES, LANES), BF16)
    zero_block = jnp.zeros((LANES, LANES), BF16)
    for e in range(2):
        lanes = slice(e * LANES, (e + 1) * LANES)
        for dr in range(3):
            w_one[dr, 3 - 3 * e, :, lanes] = zero_one
            w_two[dr, 3 - 3 * e, :, lanes] = zero_block
            for layer in range(4):
                w_mid[layer, dr, 3 - 3 * e, :, lanes] = zero_block
        for half in range(2):
            w_two[3, 2 * (1 - e) + half, :, lanes] = zero_block
    bias_f[...] = br_ref[...].astype(F32)
    zero_col = (cols + 1) * sx
    for half in range(2):
        act[half, zero_col] = jnp.zeros((segrows + 2, SEGS, LANES), BF16)

    pl.semaphore_wait(barrier, devices - 1)

    def copies(par, first, i):
        found = []
        if first:
            col_src, col_dst = wide.at[i, :, edge], halo_even.at[i]
        elif par == 0:
            col_src, col_dst = wide.at[i, 0, edge], halo_even.at[i, 0]
        else:
            col_src, col_dst = thin.at[i, edge], halo_odd.at[i]
        pick = (lambda ref: ref) if first else (lambda ref: ref.at[0])
        mine = pick(stat.at[par, i, me])
        for k, peer in enumerate(peers):
            found.append((mine, mine, stat_ss.at[par, i, k], stat_rs.at[par, i, k], peer))
        for t in range(2):
            other = lax.rem(sy + (n_sy - 1 if t == 0 else 1), n_sy)
            found.append((pick(row_send.at[i, t]), pick(row_recv.at[par, i, 1 - t]), row_ss.at[par, i, t], row_rs.at[par, i, t], {"sx": sx, "sy": other}))
            found.append((pick(cor_send.at[i, t]), pick(cor_recv.at[par, i, 1 - t]), cor_ss.at[par, i, t], cor_rs.at[par, i, t], {"sx": 1 - sx, "sy": other}))
        found.append((col_src, col_dst, col_ss.at[par, i], col_rs.at[par, i], {"sx": 1 - sx, "sy": sy}))
        return [
            pltpu.make_async_remote_copy(src_ref=src, dst_ref=dst, send_sem=ss, recv_sem=rs, device_id=peer, device_id_type=MESH)
            for src, dst, ss, rs, peer in found
        ]

    def send(par, first, i, sums):
        buf = wide if par == 0 else thin
        for half in range(2 if first else 1):
            stat[par, i, me, half] = jnp.concatenate([jnp.sum(part, axis=0, keepdims=True) for part in sums[half]], axis=0)
            for t in range(2):
                for c in range(cols):
                    where = (i, half, c) if par == 0 else (i, c)
                    tile = buf[where + (t * (segrows - 1),)].astype(F32)
                    row_send[i, t, half, pl.ds(c, 1), :] = tile[t * (SEGS - 1):t * (SEGS - 1) + 1]
                cor_send[i, t, half] = row_send[i, t, half, pl.ds(edge, 1), :]
        for copy in copies(par, first, i):
            copy.start()

    def prepare(i, _):
        slot = lax.rem(i, 2)
        land_copy(i, slot).wait()

        @pl.when(i + 1 < samples)
        def _():
            land_copy(i + 1, 1 - slot).start()

        def relayout(r, sums):
            new = []
            for half in range(2):
                block = land[slot, :, r, :, pl.ds(half * LANES, LANES)].astype(F32)
                s_one, s_two = sums[half]
                new.append((s_one + jnp.sum(block, axis=0), s_two + jnp.sum(block * block, axis=0)))
                shuffle[half] = block.reshape(SEGS * cols, LANES)
                for c in range(cols):
                    wide[i, half, c, r] = shuffle[half, pl.ds(c, SEGS, stride=cols), :].astype(BF16)
            return tuple(new)

        zero = jnp.zeros((8, LANES), F32)
        sums = lax.fori_loop(0, segrows, relayout, ((zero, zero), (zero, zero)))
        send(0, True, i, sums)
        return 0

    lax.fori_loop(0, samples, prepare, 0)
    for copy in weight_copies:
        copy.wait()

    lane = lax.broadcasted_iota(jnp.int32, (2, LANES), 1)
    seg_at = lax.broadcasted_iota(jnp.int32, (SEGS, LANES), 0)

    def group_total(x, size):
        step = 1
        while step < size:
            x = x + jnp.where((lane & step) != 0, pltpu.roll(x, step, 1), pltpu.roll(x, LANES - step, 1))
            step *= 2
        return x

    def silu_half(x, scale, shift):
        v = x * scale + shift
        return v + v * jnp.tanh(v)

    def activate(par, first, i, pair_of):
        for copy in copies(par, first, i):
            copy.wait()
        per_group = (2 if first else 1) * LANES // GROUPS
        count = pixels * per_group
        for half in range(2 if first else 1):
            total = stat[par, i, 0, half]
            for dev in range(1, devices):
                total = total + stat[par, i, dev, half]
            total = group_total(total, per_group) * (1.0 / count)
            mean, square = total[0:1], total[1:2]
            gamma, beta = pair_of(half)
            scale = gamma * lax.rsqrt(square - mean * mean + GN_EPS)
            shift = beta - mean * scale
            scale, shift = 0.5 * scale, 0.5 * shift

            def column(src, above, below, dst):
                z = silu_half(src.astype(F32), scale, shift)
                act[half, dst, 1:segrows + 1] = z.astype(BF16)
                above = jnp.where(sy > 0, silu_half(above, scale, shift), 0.0)
                below = jnp.where(sy < n_sy - 1, silu_half(below, scale, shift), 0.0)
                act[half, dst, 0] = jnp.where(seg_at == 0, above, pltpu.roll(z[segrows - 1], 1, 0)).astype(BF16)
                act[half, dst, segrows + 1] = jnp.where(seg_at == SEGS - 1, below, pltpu.roll(z[0], SEGS - 1, 0)).astype(BF16)

            def own(c, _):
                src = wide[i, half, c] if par == 0 else thin[i, c]
                column(src, row_recv[par, i, 0, half, pl.ds(c, 1), :], row_recv[par, i, 1, half, pl.ds(c, 1), :], c + 1)
                return 0

            lax.fori_loop(0, cols, own, 0)
            src = halo_even[i, half] if par == 0 else halo_odd[i]
            column(src, cor_recv[par, i, 0, half], cor_recv[par, i, 1, half], (cols + 1) * (1 - sx))

    def conv(par, first, i, weights, bias, skip, residual):
        halves = 2 if first else 1

        def pair(p, sums):
            pieces = []
            for dr in range(3):
                for j in range(4):
                    for half in range(halves):
                        pieces.append(act[half, 2 * p + j, dr:dr + segrows].reshape(px, LANES))
            if skip:
                for e in range(2):
                    for half in range(2):
                        pieces.append(wide[i, half, 2 * p + e].reshape(px, LANES))
            res = jnp.dot(jnp.concatenate(pieces, axis=1), weights(), preferred_element_type=F32)
            s_one, s_two = sums
            for e in range(2):
                y = res[:, e * LANES:(e + 1) * LANES] + bias
                if residual:
                    y = y + wide[i, 0, 2 * p + e].reshape(px, LANES).astype(F32)
                rounded = y.astype(BF16)
                if par == 0:
                    thin[i, 2 * p + e] = rounded.reshape(segrows, SEGS, LANES)
                else:
                    wide[i, 0, 2 * p + e] = rounded.reshape(segrows, SEGS, LANES)
                back = rounded.astype(F32).reshape(px // 8, 8, LANES)
                s_one = s_one + jnp.sum(back, axis=0)
                s_two = s_two + jnp.sum(back * back, axis=0)
            return s_one, s_two

        zero = jnp.zeros((8, LANES), F32)
        sums = lax.fori_loop(0, cols // 2, pair, (zero, zero))
        send(1 - par, False, i, [sums])

    def rest_pair(at):
        pair = nr_ref[at].astype(F32)
        return lambda half: (pair[0:1], pair[1:2])

    def first_pair(half):
        pair = nf_ref[:, half * LANES:(half + 1) * LANES].astype(F32)
        return pair[0:1], pair[1:2]

    def layer_one(i, _):
        activate(0, True, i, first_pair)
        conv(0, True, i, lambda: w_one[...].reshape(24 * LANES, 2 * LANES), bias_f[0:1], False, False)
        return 0

    def layer_two(i, _):
        activate(1, False, i, rest_pair(0))
        conv(1, False, i, lambda: w_two[...].reshape(16 * LANES, 2 * LANES), bias_f[1:2] + bias_f[6:7], True, False)
        return 0

    lax.fori_loop(0, samples, layer_one, 0)
    lax.fori_loop(0, samples, layer_two, 0)

    def block(k, _):
        def body(which):
            def layer(i, _):
                at = 2 * k + which
                activate(which, False, i, rest_pair(at + 1))
                conv(which, False, i, lambda: w_mid[at].reshape(12 * LANES, 2 * LANES), bias_f[pl.ds(at + 2, 1), :], False, which == 1)
                return 0
            return layer

        lax.fori_loop(0, samples, body(0), 0)
        lax.fori_loop(0, samples, body(1), 0)
        return 0

    lax.fori_loop(0, 2, block, 0)

    def head(i, _):
        activate(0, False, i, rest_pair(5))

        def column(c, _):
            pieces = []
            for dr in range(3):
                for dc in range(3):
                    pieces.append(act[0, c + dc, dr:dr + segrows].reshape(px, LANES))
            y = lax.dot_general(wo_ref[...], jnp.concatenate(pieces, axis=1), (((1,), (1,)), ((), ())), preferred_element_type=F32)
            for ch in range(3):
                out_ref[i, ch, pl.ds(c, 1), :] = y[ch:ch + 1] + bo_ref[ch:ch + 1, 0:1]
            return 0

        lax.fori_loop(0, cols, column, 0)
        return 0

    lax.fori_loop(0, samples, head, 0)


def solution(mesh):
    n_sy = mesh.shape["sy"]
    n_sx = mesh.shape["sx"]
    devices = n_sx * n_sy
    tile_spec = P("dp", "sy", "sx", None)
    replicated = P()

    def local_decode(act_in, norm_first, w_first, w_short, norm_rest, w_rest, bias_rest, w_out, bias_out):
        samples, rows, cols, chans = act_in.shape
        segrows = rows // SEGS
        act_five = act_in.reshape(samples, SEGS, segrows, cols, chans)
        head_w = jnp.pad(jnp.transpose(w_out, (3, 0, 1, 2)).reshape(3, 9 * LANES), ((0, 13), (0, 0)))
        head_b = jnp.broadcast_to(jnp.pad(bias_out.astype(F32), (0, 5))[:, None], (8, LANES))
        vmem = pl.BlockSpec(memory_space=pltpu.VMEM)
        hbm = pl.BlockSpec(memory_space=pl.ANY)
        dma = pltpu.SemaphoreType.DMA
        scratch = [
            pltpu.VMEM((samples, 2, cols, segrows, SEGS, LANES), BF16),
            pltpu.VMEM((samples, cols, segrows, SEGS, LANES), BF16),
            pltpu.VMEM((2, cols + 2, segrows + 2, SEGS, LANES), BF16),
            pltpu.VMEM((3, 4, 2 * LANES, 2 * LANES), BF16),
            pltpu.VMEM((4, 4, LANES, 2 * LANES), BF16),
            pltpu.VMEM((4, 3, 4, LANES, 2 * LANES), BF16),
            pltpu.VMEM((samples, 2, segrows, SEGS, LANES), BF16),
            pltpu.VMEM((samples, segrows, SEGS, LANES), BF16),
            pltpu.VMEM((2, SEGS, segrows, cols, chans), BF16),
            pltpu.VMEM((2, SEGS * cols, LANES), F32),
            pltpu.VMEM((7, LANES), F32),
            pltpu.VMEM((samples, 2, 2, cols, LANES), F32),
            pltpu.VMEM((2, samples, 2, 2, cols, LANES), F32),
            pltpu.VMEM((samples, 2, 2, 1, LANES), F32),
            pltpu.VMEM((2, samples, 2, 2, 1, LANES), F32),
            pltpu.VMEM((2, samples, devices, 2, 2, LANES), F32),
            dma((2,)),
            dma((40,)),
            dma((2, samples)),
            dma((2, samples)),
            dma((2, samples, 2)),
            dma((2, samples, 2)),
            dma((2, samples, 2)),
            dma((2, samples, 2)),
            dma((2, samples, devices - 1)),
            dma((2, samples, devices - 1)),
        ]
        cfg = (samples, segrows, cols, n_sx, n_sy)
        image = pl.pallas_call(
            functools.partial(decode_kernel, cfg),
            out_shape=jax.ShapeDtypeStruct((samples, 3, cols, rows), F32),
            in_specs=[hbm, vmem, hbm, hbm, vmem, hbm, vmem, vmem, vmem],
            out_specs=vmem,
            scratch_shapes=scratch,
            compiler_params=pltpu.CompilerParams(collective_id=0, has_side_effects=True, vmem_limit_bytes=67043328),
        )(act_five, norm_first, w_first, w_short, norm_rest, w_rest, bias_rest, head_w, head_b)
        image = image.reshape(samples, 3, cols, segrows, SEGS)
        return jnp.transpose(image, (0, 4, 3, 2, 1)).reshape(samples, rows, cols, 3)

    return jax.shard_map(local_decode, mesh=mesh, in_specs=(tile_spec, replicated, replicated, replicated, replicated, replicated, replicated, replicated, replicated), out_specs=tile_spec, check_vma=False)
```

time: 1290 us -> 359 us (0.28)
  matrix products: 557 us -> 0 us
  Pallas kernels: 0 us -> 346 us
  waiting for transfers between devices: 297 us -> 0 us
  other arithmetic: 185 us -> 0.66 us
  blocking collectives: 160 us -> 0 us
  starting transfers between devices: 50.7 us -> 0 us
  local copies, waits for them, and re-layouts: 28.8 us -> 11.5 us
    conv_general_dilated x7 -> x0, matrix products: 537 us -> none  [conv_tile(): lax.conv_general_dilated(add_border(act_map), kernel, (1, 1), ((0, 0), (0...]
    pallas_call x0 -> x1, Pallas kernels: none -> 346 us  [local_decode(): pl.pallas_call(functools.partial(decode_kernel, cfg), out_shape=jax.Shape...]
    ppermute x28 -> x0, waiting for transfers between devices: 297 us -> none  [the longest x7 233 us: add_border(): left_col = lax.ppermute(tall[:, :, -1:], 'sx', to_right)]
    psum x7 -> x0, blocking collectives: 160 us -> none  [group_norm_act(): totals = lax.psum(jnp.stack([sum_one, sum_two], axis=-1), ('sy', 'sx'))]
    convert_element_type x10 -> x0, other arithmetic: 126 us -> none  [the longest x7 125 us: group_norm_act(): jax.nn.silu(act_map.astype(jnp.float32) * chan_scale[:, None, None, :] +...]
    ppermute x28 -> x0, starting transfers between devices: 50.7 us -> none  [the longest x7 22.8 us: add_border(): left_col = lax.ppermute(tall[:, :, -1:], 'sx', to_right)]
    reduce_sum x15 -> x0, other arithmetic: 45.8 us -> none  [the longest x8 45.5 us: group_norm_act(): jnp.sum(act_map, axis=(1, 2), dtype=jnp.float32)]
    dot_general x1 -> x0, matrix products: 20.4 us -> none  [local_decode(): jnp.einsum('nhwc,cd->nhwd', act_in, w_short, preferred_element_type=jnp.f...]
  transfers between devices with their start and end apart: 28 -> 0, of which waited for: 21 -> 0; matrix products, arithmetic and copies ran while one was open for 2% -> 0% of each run, Pallas kernels for 0% -> 0%
where the time goes in v1:
time: 359 us; the launch traced here: 358 us
  Pallas kernels  346 us (96%)
  local copies, waits for them, and re-layouts  11.5 us (3%)
    pallas_call x1, Pallas kernels, local_decode(): pl.pallas_call(functools.partial(decode_kernel, cfg), out_shape=jax.Shape...  346 us

profile of v1, /device:TPU:0, one launch (start us, length us, event | category | flops | bytes accessed | tf_op | source)
XLA Modules:
  0.0 358.4 jit_solution(6228186134501869902)
XLA Ops:
  0.0 0.7 pad_convert_fusion
  0.7 0.7 broadcast_in_dim.2.bo_ref
  1.3 1.3 pad.11.wo_ref
  2.6 346.2 %shard_map.91 = f32[12,3,8,512]{3,2,1,0:T(8,128)} custom-call(bf16[12,16,32,8,256]{4,3,2,1,0:T(8,128)(2,1)} %bitcast.11, bf16[2,256]{1,0:T(2,128)(2,1)} %nf_ref.1, bf16[3,3,256,128]{3,2,1,0:T(8,128)(2,1)} %wf_hbm.1, bf16[256,128]{1,0:T(8,128)(2,1)} %ws_hbm.1, bf16[6,2,128]{2,1,0:T(2,128)(2,1)} %nr_ref.1, bf16[5,3,3,128,128]{4,3,2,1,0:T(8,128)(2,1)} %wr_hbm.1, ...), custom_call_target="tpu_custom_call" | custom-call | tf_op jit(solution)/shard_map/pallas_call | solution.py:318
  348.9 4.1 %reshape.15 = f32[12,3,8,32,16]{4,3,2,1,0:T(8,128)} reshape(f32[12,3,8,512]{3,2,1,0:T(8,128)} %shard_map.91) | data formatting | bytes 1179648 | tf_op jit(solution)/shard_map/reshape | solution.py:326
  352.9 3.8 %copy.11 = f32[12,16,32,8,3]{2,1,3,4,0:T(8,128)S(1)} copy(f32[12,16,32,8,3]{1,2,3,4,0:T(8,128)} %bitcast.12) | data formatting | bytes 1179648 | tf_op jit(solution)/shard_map/transpose | solution.py:327
  356.7 1.7 reshape.16

commit v2 on v1

v2 whole, which is shorter than its diff:
```python
import functools

import jax
import jax.numpy as jnp
from jax import lax
from jax.experimental import pallas as pl
from jax.experimental.pallas import tpu as pltpu
from jax.sharding import PartitionSpec as P

GROUPS = 32
GN_EPS = 1e-6
LANES = 128
SEGS = 16
MESH = pl.DeviceIdType.MESH
F32 = jnp.float32
BF16 = jnp.bfloat16


def decode_kernel(cfg, a_hbm, nf_ref, wf_hbm, ws_hbm, nr_ref, wr_hbm, br_ref, wo_ref, bo_ref, out_ref,
                  wide, thin, act_a, act_b, w_one, w_two, w_mid, halo_even, halo_odd, land, shuffle, bias_f,
                  row_send, row_recv, cor_send, cor_recv, stat, tally, head_f, head_w, order, part, image, q_send, q_recv,
                  land_sem, w_sem, col_ss, col_rs, small_ss, small_rs, q_ss, q_rs):
    samples, segrows, cols, n_sx, n_sy = cfg
    devices = n_sx * n_sy
    px = segrows * SEGS
    sx = lax.axis_index("sx")
    sy = lax.axis_index("sy")
    me = sx * n_sy + sy
    edge = (cols - 1) * (1 - sx)
    pixels = segrows * SEGS * cols * devices
    acts = (act_a, act_b)

    barrier = pltpu.get_barrier_semaphore()
    peers = []
    for k in range(1, devices):
        peers.append({"sx": lax.rem(sx + k // n_sy, n_sx), "sy": lax.rem(sy + k % n_sy, n_sy)})
    for peer in peers:
        pl.semaphore_signal(barrier, inc=1, device_id=peer, device_id_type=MESH)

    def land_copy(i, slot):
        return pltpu.make_async_copy(a_hbm.at[i], land.at[slot], land_sem.at[slot])

    land_copy(0, 0).start()

    weight_copies = []
    for e in range(2):
        lanes = pl.ds(e * LANES, LANES)
        for dr in range(3):
            weight_copies.append((wf_hbm.at[dr], w_one.at[dr, pl.ds(e, 3), :, lanes]))
            weight_copies.append((wr_hbm.at[0, dr], w_two.at[dr, pl.ds(e, 3), :, lanes]))
            for layer in range(4):
                weight_copies.append((wr_hbm.at[layer + 1, dr], w_mid.at[layer, dr, pl.ds(e, 3), :, lanes]))
        for half in range(2):
            weight_copies.append((ws_hbm.at[pl.ds(half * LANES, LANES)], w_two.at[3, 2 * e + half, :, lanes]))
    weight_copies = [pltpu.make_async_copy(src, dst, w_sem.at[n]) for n, (src, dst) in enumerate(weight_copies)]

    pl.semaphore_wait(barrier, devices - 1)

    def column_copy(par, first, i):
        if first:
            src, dst = wide.at[i, :, edge], halo_even.at[i]
        elif par == 0:
            src, dst = wide.at[i, 0, edge], halo_even.at[i, 0]
        else:
            src, dst = thin.at[i, edge], halo_odd.at[i]
        return pltpu.make_async_remote_copy(
            src_ref=src, dst_ref=dst, send_sem=col_ss.at[par, i], recv_sem=col_rs.at[par, i],
            device_id={"sx": 1 - sx, "sy": sy}, device_id_type=MESH)

    def small_copies(par, first, i):
        pick = (lambda ref: ref) if first else (lambda ref: ref.at[0])
        mine = pick(stat.at[par, i, me])
        found = [(mine, mine, peer) for peer in peers]
        for t in range(2):
            other = lax.rem(sy + (n_sy - 1 if t == 0 else 1), n_sy)
            found.append((pick(row_send.at[i, t]), pick(row_recv.at[par, i, 1 - t]), {"sx": sx, "sy": other}))
            found.append((pick(cor_send.at[i, t]), pick(cor_recv.at[par, i, 1 - t]), {"sx": 1 - sx, "sy": other}))
        return [
            pltpu.make_async_remote_copy(src_ref=src, dst_ref=dst, send_sem=small_ss.at[par, i], recv_sem=small_rs.at[par, i], device_id=peer, device_id_type=MESH)
            for src, dst, peer in found
        ]

    def await_copies(par, first, i, with_column):
        size = tally if first else tally.at[0]
        pltpu.make_async_copy(size, size, small_ss.at[par, i]).wait()
        pltpu.make_async_copy(size, size, small_rs.at[par, i]).wait()
        if with_column:
            column_copy(par, first, i).wait()

    def send(par, first, i, sums, with_column):
        buf = wide if par == 0 else thin
        for half in range(2 if first else 1):
            stat[par, i, me, half] = jnp.concatenate([jnp.sum(part_sum, axis=0, keepdims=True) for part_sum in sums[half]], axis=0)
            for t in range(2):
                for c in range(cols):
                    at = (i, half, c) if par == 0 else (i, c)
                    tile = buf[at + (t * (segrows - 1),)].astype(F32)
                    row_send[i, t, half, pl.ds(c, 1), :] = tile[t * (SEGS - 1):t * (SEGS - 1) + 1]
                cor_send[i, t, half] = row_send[i, t, half, pl.ds(edge, 1), :]
        for copy in small_copies(par, first, i):
            copy.start()
        if with_column:
            column_copy(par, first, i).start()

    def prepare(i, _):
        slot = lax.rem(i, 2)
        land_copy(i, slot).wait()

        @pl.when(i + 1 < samples)
        def _():
            land_copy(i + 1, 1 - slot).start()

        def relayout(r, sums):
            new = []
            for half in range(2):
                block = land[slot, :, r, :, pl.ds(half * LANES, LANES)].astype(F32)
                s_one, s_two = sums[half]
                new.append((s_one + jnp.sum(block, axis=0), s_two + jnp.sum(block * block, axis=0)))
                shuffle[half] = block.reshape(SEGS * cols, LANES)
                for c in range(cols):
                    wide[i, half, c, r] = shuffle[half, pl.ds(c, SEGS, stride=cols), :].astype(BF16)
            return tuple(new)

        zero = jnp.zeros((8, LANES), F32)
        sums = lax.fori_loop(0, segrows, relayout, ((zero, zero), (zero, zero)))
        send(0, True, i, sums, True)
        return 0

    prepare(0, 0)
    for copy in weight_copies:
        copy.start()
    zero_one = jnp.zeros((2 * LANES, LANES), BF16)
    zero_block = jnp.zeros((LANES, LANES), BF16)
    for e in range(2):
        lanes = slice(e * LANES, (e + 1) * LANES)
        for dr in range(3):
            w_one[dr, 3 - 3 * e, :, lanes] = zero_one
            w_two[dr, 3 - 3 * e, :, lanes] = zero_block
            for layer in range(4):
                w_mid[layer, dr, 3 - 3 * e, :, lanes] = zero_block
        for half in range(2):
            w_two[3, 2 * (1 - e) + half, :, lanes] = zero_block
    bias_f[...] = br_ref[...].astype(F32)
    zero_col = (cols + 1) * sx
    for half in range(2):
        for buf in acts:
            buf[half, zero_col] = jnp.zeros((segrows + 2, SEGS, LANES), BF16)
    head_f[...] = jnp.zeros(head_f.shape, F32)
    for dr in range(3):
        for kc in range(3):
            head_f[kc * 8:kc * 8 + 3, dr * LANES:(dr + 1) * LANES] = wo_ref[dr, kc].astype(F32)
    head_w[...] = head_f[...].astype(BF16)
    came = lax.broadcasted_iota(jnp.int32, (px, px), 0)
    goes = lax.broadcasted_iota(jnp.int32, (px, px), 1)
    order[...] = jnp.where(goes == lax.rem(came, SEGS) * segrows + lax.div(came, SEGS), 1.0, 0.0).astype(BF16)
    part[0, 0] = jnp.zeros((8, px), F32)
    part[cols + 1, 2] = jnp.zeros((8, px), F32)

    lax.fori_loop(1, samples, prepare, 0)
    for copy in weight_copies:
        copy.wait()

    lane = lax.broadcasted_iota(jnp.int32, (2, LANES), 1)
    seg_at = lax.broadcasted_iota(jnp.int32, (SEGS, LANES), 0)

    def group_total(x, size):
        step = 1
        while step < size:
            x = x + jnp.where((lane & step) != 0, pltpu.roll(x, step, 1), pltpu.roll(x, LANES - step, 1))
            step *= 2
        return x

    def silu_half(x, scale, shift):
        v = x * scale + shift
        return v + v * jnp.tanh(v)

    def norms(par, first, i, pair_of):
        per_group = (2 if first else 1) * LANES // GROUPS
        count = pixels * per_group
        found = []
        for half in range(2 if first else 1):
            total = stat[par, i, 0, half]
            for dev in range(1, devices):
                total = total + stat[par, i, dev, half]
            total = group_total(total, per_group) * (1.0 / count)
            mean, square = total[0:1], total[1:2]
            gamma, beta = pair_of(half)
            scale = gamma * lax.rsqrt(square - mean * mean + GN_EPS)
            shift = beta - mean * scale
            found.append((0.5 * scale, 0.5 * shift))
        return found

    def column(src, above, below, dst, scale, shift):
        z = silu_half(src.astype(F32), scale, shift)
        dst[1:segrows + 1] = z.astype(BF16)
        above = jnp.where(sy > 0, silu_half(above, scale, shift), 0.0)
        below = jnp.where(sy < n_sy - 1, silu_half(below, scale, shift), 0.0)
        dst[0] = jnp.where(seg_at == 0, above, pltpu.roll(z[segrows - 1], 1, 0)).astype(BF16)
        dst[segrows + 1] = jnp.where(seg_at == SEGS - 1, below, pltpu.roll(z[0], SEGS - 1, 0)).astype(BF16)

    def own_column(par, i, half, c, dst, scale, shift):
        src = wide[i, half, c] if par == 0 else thin[i, c]
        column(src, row_recv[par, i, 0, half, pl.ds(c, 1), :], row_recv[par, i, 1, half, pl.ds(c, 1), :], dst, scale, shift)

    def halo_column(par, first, i, buf, factors):
        for half, (scale, shift) in enumerate(factors):
            src = halo_even[i, half] if par == 0 else halo_odd[i]
            column(src, cor_recv[par, i, 0, half], cor_recv[par, i, 1, half], buf.at[half, (cols + 1) * (1 - sx)], scale, shift)

    def run_layer(par, first, pair_of, weights, bias, skip, residual, last, after):
        halves = 2 if first else 1

        await_copies(par, first, 0, True)
        start = norms(par, first, 0, pair_of)
        halo_column(par, first, 0, act_a, start)

        def own(c, _):
            for half, (scale, shift) in enumerate(start):
                own_column(par, 0, half, c, act_a.at[half, c + 1], scale, shift)
            return 0

        lax.fori_loop(0, cols, own, 0)

        def step(i, s):
            now, later = acts[s], acts[1 - s]
            if s == 0:
                ahead = i + 1
                await_copies(par, first, ahead, True)
            else:
                ahead = jnp.minimum(i + 1, samples - 1)

                @pl.when(i + 1 < samples)
                def _():
                    await_copies(par, first, ahead, True)

            factors = norms(par, first, ahead, pair_of)
            halo_column(par, first, ahead, later, factors)

            def pair(p, sums):
                pieces = []
                for dr in range(3):
                    for j in range(4):
                        for half in range(halves):
                            pieces.append(now[half, 2 * p + j, dr:dr + segrows].reshape(px, LANES))
                if skip:
                    for e in range(2):
                        for half in range(2):
                            pieces.append(wide[i, half, 2 * p + e].reshape(px, LANES))
                res = jnp.dot(jnp.concatenate(pieces, axis=1), weights(), preferred_element_type=F32)
                for half, (scale, shift) in enumerate(factors):
                    for e in range(2):
                        own_column(par, ahead, half, 2 * p + e, later.at[half, 2 * p + e + 1], scale, shift)
                s_one, s_two = sums
                for e in range(2):
                    y = res[:, e * LANES:(e + 1) * LANES] + bias
                    if residual:
                        y = y + wide[i, 0, 2 * p + e].reshape(px, LANES).astype(F32)
                    rounded = y.astype(BF16)
                    if par == 0:
                        thin[i, 2 * p + e] = rounded.reshape(segrows, SEGS, LANES)
                    else:
                        wide[i, 0, 2 * p + e] = rounded.reshape(segrows, SEGS, LANES)
                    back = rounded.astype(F32).reshape(px // 8, 8, LANES)
                    s_one = s_one + jnp.sum(back, axis=0)
                    s_two = s_two + jnp.sum(back * back, axis=0)
                return s_one, s_two

            zero = jnp.zeros((8, LANES), F32)
            sums = lax.fori_loop(0, cols // 2, pair, (zero, zero))
            send(1 - par, False, i, [sums], not last)
            after(i)

        def two(t, _):
            step(2 * t, 0)
            step(2 * t + 1, 1)
            return 0

        lax.fori_loop(0, samples // 2, two, 0)

    def rest_pair(at):
        def pair_of(half):
            pair = nr_ref[at].astype(F32)
            return pair[0:1], pair[1:2]
        return pair_of

    def first_pair(half):
        pair = nf_ref[:, half * LANES:(half + 1) * LANES].astype(F32)
        return pair[0:1], pair[1:2]

    def edge_copy(i):
        return pltpu.make_async_remote_copy(
            src_ref=q_send.at[i], dst_ref=q_recv.at[i], send_sem=q_ss.at[i], recv_sem=q_rs.at[i],
            device_id={"sx": 1 - sx, "sy": sy}, device_id_type=MESH)

    def head_products(i):
        await_copies(0, False, i, False)
        (scale, shift), = norms(0, False, i, rest_pair(5))
        buf = act_b.at[1]

        def column_product(c, _):
            own_column(0, i, 0, c, buf.at[c + 1], scale, shift)
            pieces = [buf[c + 1, dr:dr + segrows].reshape(px, LANES) for dr in range(3)]
            prod = lax.dot_general(head_w[...], jnp.concatenate(pieces, axis=1), (((1,), (1,)), ((), ())), preferred_element_type=F32)
            for kc in range(3):
                part[c + 1, kc] = prod[kc * 8:kc * 8 + 8]
            return 0

        lax.fori_loop(0, cols, column_product, 0)
        q_send[i] = part[edge + 1, 2 * sx][0:4]
        edge_copy(i).start()
        slot = lax.rem(i, 4)
        for c in range(cols):
            y = part[c, 0] + part[c + 1, 1] + part[c + 2, 2]
            for ch in range(3):
                image[slot, ch * cols + c:ch * cols + c + 1, :] = y[ch:ch + 1]

    def head_finish(i):
        edge_copy(i).wait()
        slot = lax.rem(i, 4)
        for ch in range(3):
            at = pl.ds(ch * cols + edge, 1)
            image[slot, at, :] = image[slot, at, :] + q_recv[i][ch:ch + 1]
        y = image[slot]
        high = y.astype(BF16).astype(F32)
        rest = y - high
        mid = rest.astype(BF16).astype(F32)
        split = jnp.concatenate([high, mid, rest - mid], axis=0).astype(BF16)
        moved = jnp.dot(split, order[...], preferred_element_type=F32)
        n = 3 * cols
        moved = moved[0:n] + (moved[n:2 * n] + moved[2 * n:3 * n])
        shift = bo_ref[...].astype(F32)
        for ch in range(3):
            out_ref[i, ch] = moved[ch * cols:(ch + 1) * cols] + shift[0:1, ch:ch + 1]

    def nothing(i):
        pass

    def head(i):
        @pl.when(i >= 2)
        def _():
            head_products(i - 2)

        @pl.when(i >= 4)
        def _():
            head_finish(i - 4)

    run_layer(0, True, first_pair, lambda: w_one[...].reshape(24 * LANES, 2 * LANES), bias_f[0:1], False, False, False, nothing)
    run_layer(1, False, rest_pair(0), lambda: w_two[...].reshape(16 * LANES, 2 * LANES), bias_f[1:2] + bias_f[6:7], True, False, False, nothing)
    for at in range(4):
        weights = functools.partial(lambda n: w_mid[n].reshape(12 * LANES, 2 * LANES), at)
        run_layer(at % 2, False, rest_pair(at + 1), weights, bias_f[at + 2:at + 3], False, at % 2 == 1, at == 3, head if at == 3 else nothing)

    def tail(i, _):
        @pl.when(i < samples + 2)
        def _():
            head_products(i - 2)

        head_finish(i - 4)
        return 0

    lax.fori_loop(samples, samples + 4, tail, 0)


def solution(mesh):
    n_sy = mesh.shape["sy"]
    n_sx = mesh.shape["sx"]
    devices = n_sx * n_sy
    tile_spec = P("dp", "sy", "sx", None)
    replicated = P()

    def local_decode(act_in, norm_first, w_first, w_short, norm_rest, w_rest, bias_rest, w_out, bias_out):
        samples, rows, cols, chans = act_in.shape
        segrows = rows // SEGS
        act_five = act_in.reshape(samples, SEGS, segrows, cols, chans)
        w_head = jnp.transpose(w_out, (0, 1, 3, 2))
        vmem = pl.BlockSpec(memory_space=pltpu.VMEM)
        hbm = pl.BlockSpec(memory_space=pl.ANY)
        dma = pltpu.SemaphoreType.DMA
        scratch = [
            pltpu.VMEM((samples, 2, cols, segrows, SEGS, LANES), BF16),
            pltpu.VMEM((samples, cols, segrows, SEGS, LANES), BF16),
            pltpu.VMEM((2, cols + 2, segrows + 2, SEGS, LANES), BF16),
            pltpu.VMEM((2, cols + 2, segrows + 2, SEGS, LANES), BF16),
            pltpu.VMEM((3, 4, 2 * LANES, 2 * LANES), BF16),
            pltpu.VMEM((4, 4, LANES, 2 * LANES), BF16),
            pltpu.VMEM((4, 3, 4, LANES, 2 * LANES), BF16),
            pltpu.VMEM((samples, 2, segrows, SEGS, LANES), BF16),
            pltpu.VMEM((samples, segrows, SEGS, LANES), BF16),
            pltpu.VMEM((2, SEGS, segrows, cols, chans), BF16),
            pltpu.VMEM((2, SEGS * cols, LANES), F32),
            pltpu.VMEM((7, LANES), F32),
            pltpu.VMEM((samples, 2, 2, cols, LANES), F32),
            pltpu.VMEM((2, samples, 2, 2, cols, LANES), F32),
            pltpu.VMEM((samples, 2, 2, 1, LANES), F32),
            pltpu.VMEM((2, samples, 2, 2, 1, LANES), F32),
            pltpu.VMEM((2, samples, devices, 2, 2, LANES), F32),
            pltpu.VMEM((2, 2 * (devices - 1) + 2 * cols + 2, LANES), F32),
            pltpu.VMEM((32, 3 * LANES), F32),
            pltpu.VMEM((32, 3 * LANES), BF16),
            pltpu.VMEM((segrows * SEGS, segrows * SEGS), BF16),
            pltpu.VMEM((cols + 2, 3, 8, segrows * SEGS), F32),
            pltpu.VMEM((4, 3 * cols, segrows * SEGS), F32),
            pltpu.VMEM((samples, 4, segrows * SEGS), F32),
            pltpu.VMEM((samples, 4, segrows * SEGS), F32),
            dma((2,)),
            dma((40,)),
            dma((2, samples)),
            dma((2, samples)),
            dma((2, samples)),
            dma((2, samples)),
            dma((samples,)),
            dma((samples,)),
        ]
        cfg = (samples, segrows, cols, n_sx, n_sy)
        image = pl.pallas_call(
            functools.partial(decode_kernel, cfg),
            out_shape=jax.ShapeDtypeStruct((samples, 3, cols, rows), F32),
            in_specs=[hbm, vmem, hbm, hbm, vmem, hbm, vmem, vmem, vmem],
            out_specs=vmem,
            scratch_shapes=scratch,
            compiler_params=pltpu.CompilerParams(collective_id=0, has_side_effects=True, vmem_limit_bytes=67043328),
        )(act_five, norm_first, w_first, w_short, norm_rest, w_rest, bias_rest, w_head, bias_out.reshape(1, 3))
        return jnp.transpose(image, (0, 3, 2, 1))

    return jax.shard_map(local_decode, mesh=mesh, in_specs=(tile_spec, replicated, replicated, replicated, replicated, replicated, replicated, replicated, replicated), out_specs=tile_spec, check_vma=False)
```

time: 359 us -> 320 us (0.89)
  Pallas kernels: 346 us -> 317 us
  local copies, waits for them, and re-layouts: 11.5 us -> 1.92 us
    pallas_call x1, Pallas kernels: 346 us -> 317 us  [local_decode(): pl.pallas_call(functools.partial(decode_kernel, cfg), out_shape=jax.Shape...]
    reshape x2 -> x0, local copies, waits for them, and re-layouts: 5.78 us -> none  [the longest x1 4.07 us: local_decode(): image = image.reshape(samples, 3, cols, segrows, SEGS)]
    transpose x1 -> x0, local copies, waits for them, and re-layouts: 3.75 us -> none  [local_decode(): return jnp.transpose(image, (0, 4, 3, 2, 1)).reshape(samples, rows, cols, 3)]
where the time goes in v2:
time: 320 us; the launch traced here: 319 us
  Pallas kernels  317 us (99%)
    pallas_call x1, Pallas kernels, local_decode(): pl.pallas_call(functools.partial(decode_kernel, cfg), out_shape=jax.Shape...  317 us

profile of v2, /device:TPU:0, one launch (start us, length us, event | category | flops | bytes accessed | tf_op | source)
XLA Modules:
  0.0 319.1 jit_solution(12714362978352966442)
XLA Ops:
  0.0 317.2 %shard_map.91 = f32[12,3,8,512]{3,2,1,0:T(8,128)} custom-call(bf16[12,16,32,8,256]{4,3,2,1,0:T(8,128)(2,1)} %bitcast.4, bf16[2,256]{1,0:T(2,128)(2,1)} %nf_ref.1, bf16[3,3,256,128]{3,2,1,0:T(8,128)(2,1)} %wf_hbm.1, bf16[256,128]{1,0:T(8,128)(2,1)} %ws_hbm.1, bf16[6,2,128]{2,1,0:T(2,128)(2,1)} %nr_ref.1, bf16[5,3,3,128,128]{4,3,2,1,0:T(8,128)(2,1)} %wr_hbm.1, ...), custom_call_target="tpu_custom_call" | custom-call | tf_op jit(solution)/shard_map/pallas_call | solution.py:415
  317.2 1.9 copy.11

commit v3 on v2

--- a/solution.py
+++ b/solution.py
@@ -9,6 +9,9 @@
 
 GROUPS = 32
 GN_EPS = 1e-6
+DEFER = 7
+HEAD_LAG = 4
+EDGE_LAG = 6
 LANES = 128
 SEGS = 16
 MESH = pl.DeviceIdType.MESH
@@ -148,7 +151,9 @@
     head_f[...] = jnp.zeros(head_f.shape, F32)
     for dr in range(3):
         for kc in range(3):
-            head_f[kc * 8:kc * 8 + 3, dr * LANES:(dr + 1) * LANES] = wo_ref[dr, kc].astype(F32)
+            for e in range(2):
+                at = 72 * e + 24 * dr + 8 * kc
+                head_f[at:at + 3, e * LANES:(e + 1) * LANES] = wo_ref[dr, kc].astype(F32)
     head_w[...] = head_f[...].astype(BF16)
     came = lax.broadcasted_iota(jnp.int32, (px, px), 0)
     goes = lax.broadcasted_iota(jnp.int32, (px, px), 1)
@@ -236,38 +241,54 @@
             factors = norms(par, first, ahead, pair_of)
             halo_column(par, first, ahead, later, factors)
 
-            def pair(p, sums):
-                pieces = []
-                for dr in range(3):
-                    for j in range(4):
-                        for half in range(halves):
-                            pieces.append(now[half, 2 * p + j, dr:dr + segrows].reshape(px, LANES))
-                if skip:
+            def quad(t, sums):
+                rows_of = []
+                for q in range(2):
+                    p = 2 * t + q
+                    pieces = []
+                    for dr in range(3):
+                        for j in range(4):
+                            for half in range(halves):
+                                pieces.append(now[half, 2 * p + j, dr:dr + segrows].reshape(px, LANES))
+                    if skip:
+                        for e in range(2):
+                            for half in range(2):
+                                pieces.append(wide[i, half, 2 * p + e].reshape(px, LANES))
+                    rows_of.append(jnp.concatenate(pieces, axis=1))
+                res = jnp.dot(jnp.concatenate(rows_of, axis=0), weights(), preferred_element_type=F32)
+                for half, (scale, shift) in enumerate(factors):
+                    for e in range(4):
+                        own_column(par, ahead, half, 4 * t + e, later.at[half, 4 * t + e + 1], scale, shift)
+                s_one, s_two = sums
+                for q in range(2):
                     for e in range(2):
-                        for half in range(2):
-                            pieces.append(wide[i, half, 2 * p + e].reshape(px, LANES))
-                res = jnp.dot(jnp.concatenate(pieces, axis=1), weights(), preferred_element_type=F32)
-                for half, (scale, shift) in enumerate(factors):
-                    for e in range(2):
-                        own_column(par, ahead, half, 2 * p + e, later.at[half, 2 * p + e + 1], scale, shift)
-                s_one, s_two = sums
-                for e in range(2):
-                    y = res[:, e * LANES:(e + 1) * LANES] + bias
-                    if residual:
-                        y = y + wide[i, 0, 2 * p + e].reshape(px, LANES).astype(F32)
-                    rounded = y.astype(BF16)
-                    if par == 0:
-                        thin[i, 2 * p + e] = rounded.reshape(segrows, SEGS, LANES)
-                    else:
-                        wide[i, 0, 2 * p + e] = rounded.reshape(segrows, SEGS, LANES)
-                    back = rounded.astype(F32).reshape(px // 8, 8, LANES)
-                    s_one = s_one + jnp.sum(back, axis=0)
-                    s_two = s_two + jnp.sum(back * back, axis=0)
+                        c = 4 * t + 2 * q + e
+                        y = res[q * px:(q + 1) * px, e * LANES:(e + 1) * LANES] + bias
+                        if residual:
+                            y = y + wide[i, 0, c].reshape(px, LANES).astype(F32)
+                        rounded = y.astype(BF16)
+                        if par == 0:
+                            thin[i, c] = rounded.reshape(segrows, SEGS, LANES)
+                        else:
+                            wide[i, 0, c] = rounded.reshape(segrows, SEGS, LANES)
+                        back = rounded.astype(F32).reshape(px // 8, 8, LANES)
+                        s_one = s_one + jnp.sum(back, axis=0)
+                        s_two = s_two + jnp.sum(back * back, axis=0)
                 return s_one, s_two
 
             zero = jnp.zeros((8, LANES), F32)
-            sums = lax.fori_loop(0, cols // 2, pair, (zero, zero))
-            send(1 - par, False, i, [sums], not last)
+            sums = lax.fori_loop(0, cols // 4, quad, (zero, zero))
+            send(1 - par, False, i, [sums], False)
+            if not last:
+                @pl.when(i >= DEFER)
+                def _():
+                    column_copy(1 - par, False, i - DEFER).start()
+
+            if not first:
+                @pl.when(i < DEFER)
+                def _():
+                    column_copy(par, False, i + samples - DEFER).start()
+
             after(i)
 
         def two(t, _):
@@ -297,15 +318,15 @@
         (scale, shift), = norms(0, False, i, rest_pair(5))
         buf = act_b.at[1]
 
-        def column_product(c, _):
-            own_column(0, i, 0, c, buf.at[c + 1], scale, shift)
-            pieces = [buf[c + 1, dr:dr + segrows].reshape(px, LANES) for dr in range(3)]
-            prod = lax.dot_general(head_w[...], jnp.concatenate(pieces, axis=1), (((1,), (1,)), ((), ())), preferred_element_type=F32)
-            for kc in range(3):
-                part[c + 1, kc] = prod[kc * 8:kc * 8 + 8]
-            return 0
-
-        lax.fori_loop(0, cols, column_product, 0)
+        for c in range(0, cols, 2):
+            for e in range(2):
+                own_column(0, i, 0, c + e, buf.at[c + e + 1], scale, shift)
+            both = jnp.concatenate([buf[c + e + 1].reshape(px + 2 * SEGS, LANES) for e in range(2)], axis=1)
+            prod = lax.dot_general(head_w[...], both, (((1,), (1,)), ((), ())), preferred_element_type=F32)
+            for e in range(2):
+                for kc in range(3):
+                    at = [72 * e + 24 * dr + 8 * kc for dr in range(3)]
+                    part[c + e + 1, kc] = sum(prod[at[dr]:at[dr] + 8, dr * SEGS:dr * SEGS + px] for dr in range(3))
         q_send[i] = part[edge + 1, 2 * sx][0:4]
         edge_copy(i).start()
         slot = lax.rem(i, 4)
@@ -336,13 +357,13 @@
         pass
 
     def head(i):
-        @pl.when(i >= 2)
+        @pl.when(i >= HEAD_LAG)
         def _():
-            head_products(i - 2)
-
-        @pl.when(i >= 4)
+            head_products(i - HEAD_LAG)
+
+        @pl.when(i >= EDGE_LAG)
         def _():
-            head_finish(i - 4)
+            head_finish(i - EDGE_LAG)
 
     run_layer(0, True, first_pair, lambda: w_one[...].reshape(24 * LANES, 2 * LANES), bias_f[0:1], False, False, False, nothing)
     run_layer(1, False, rest_pair(0), lambda: w_two[...].reshape(16 * LANES, 2 * LANES), bias_f[1:2] + bias_f[6:7], True, False, False, nothing)
@@ -351,14 +372,14 @@
         run_layer(at % 2, False, rest_pair(at + 1), weights, bias_f[at + 2:at + 3], False, at % 2 == 1, at == 3, head if at == 3 else nothing)
 
     def tail(i, _):
-        @pl.when(i < samples + 2)
+        @pl.when(i < samples + HEAD_LAG)
         def _():
-            head_products(i - 2)
-
-        head_finish(i - 4)
+            head_products(i - HEAD_LAG)
+
+        head_finish(i - EDGE_LAG)
         return 0
 
-    lax.fori_loop(samples, samples + 4, tail, 0)
+    lax.fori_loop(samples, samples + EDGE_LAG, tail, 0)
 
 
 def solution(mesh):
@@ -395,8 +416,8 @@
             pltpu.VMEM((2, samples, 2, 2, 1, LANES), F32),
             pltpu.VMEM((2, samples, devices, 2, 2, LANES), F32),
             pltpu.VMEM((2, 2 * (devices - 1) + 2 * cols + 2, LANES), F32),
-            pltpu.VMEM((32, 3 * LANES), F32),
-            pltpu.VMEM((32, 3 * LANES), BF16),
+            pltpu.VMEM((144, 2 * LANES), F32),
+            pltpu.VMEM((144, 2 * LANES), BF16),
             pltpu.VMEM((segrows * SEGS, segrows * SEGS), BF16),
             pltpu.VMEM((cols + 2, 3, 8, segrows * SEGS), F32),
             pltpu.VMEM((4, 3 * cols, segrows * SEGS), F32),

time: 320 us -> 285 us (0.89)
  Pallas kernels: 317 us -> 282 us
    pallas_call x1, Pallas kernels: 317 us -> 282 us  [local_decode(): pl.pallas_call(functools.partial(decode_kernel, cfg), out_shape=jax.Shape...]
where the time goes in v3:
time: 285 us; the launch traced here: 284 us
  Pallas kernels  282 us (99%)
    pallas_call x1, Pallas kernels, local_decode(): pl.pallas_call(functools.partial(decode_kernel, cfg), out_shape=jax.Shape...  282 us

profile of v3, /device:TPU:0, one launch (start us, length us, event | category | flops | bytes accessed | tf_op | source)
XLA Modules:
  0.0 284.4 jit_solution(13630781083642201928)
XLA Ops:
  0.0 282.5 %shard_map.91 = f32[12,3,8,512]{3,2,1,0:T(8,128)} custom-call(bf16[12,16,32,8,256]{4,3,2,1,0:T(8,128)(2,1)} %bitcast.4, bf16[2,256]{1,0:T(2,128)(2,1)} %nf_ref.1, bf16[3,3,256,128]{3,2,1,0:T(8,128)(2,1)} %wf_hbm.1, bf16[256,128]{1,0:T(8,128)(2,1)} %ws_hbm.1, bf16[6,2,128]{2,1,0:T(2,128)(2,1)} %nr_ref.1, bf16[5,3,3,128,128]{4,3,2,1,0:T(8,128)(2,1)} %wr_hbm.1, ...), custom_call_target="tpu_custom_call" | custom-call | tf_op jit(solution)/shard_map/pallas_call | solution.py:436
  282.5 1.9 copy.11

commit v4 on v3

--- a/solution.py
+++ b/solution.py
@@ -9,9 +9,9 @@
 
 GROUPS = 32
 GN_EPS = 1e-6
-DEFER = 7
-HEAD_LAG = 4
-EDGE_LAG = 6
+DEFER = 8
+HEAD_LAG = 3
+EDGE_LAG = 5
 LANES = 128
 SEGS = 16
 MESH = pl.DeviceIdType.MESH
@@ -21,7 +21,7 @@
 
 def decode_kernel(cfg, a_hbm, nf_ref, wf_hbm, ws_hbm, nr_ref, wr_hbm, br_ref, wo_ref, bo_ref, out_ref,
                   wide, thin, act_a, act_b, w_one, w_two, w_mid, halo_even, halo_odd, land, shuffle, bias_f,
-                  row_send, row_recv, cor_send, cor_recv, stat, tally, head_f, head_w, order, part, image, q_send, q_recv,
+                  row_send, row_recv, cor_send, cor_recv, stat, tally, head_f, head_w, order, image, q_send, q_recv,
                   land_sem, w_sem, col_ss, col_rs, small_ss, small_rs, q_ss, q_rs):
     samples, segrows, cols, n_sx, n_sy = cfg
     devices = n_sx * n_sy
@@ -43,7 +43,12 @@
     def land_copy(i, slot):
         return pltpu.make_async_copy(a_hbm.at[i], land.at[slot], land_sem.at[slot])
 
-    land_copy(0, 0).start()
+    def land_start(i, slot):
+        for at in range(0, SEGS, 2):
+            rows = pl.ds(at, 2)
+            pltpu.make_async_copy(a_hbm.at[i, rows], land.at[slot, rows], land_sem.at[slot]).start()
+
+    land_start(0, 0)
 
     weight_copies = []
     for e in range(2):
@@ -56,8 +61,6 @@
         for half in range(2):
             weight_copies.append((ws_hbm.at[pl.ds(half * LANES, LANES)], w_two.at[3, 2 * e + half, :, lanes]))
     weight_copies = [pltpu.make_async_copy(src, dst, w_sem.at[n]) for n, (src, dst) in enumerate(weight_copies)]
-
-    pl.semaphore_wait(barrier, devices - 1)
 
     def column_copy(par, first, i):
         if first:
@@ -105,13 +108,13 @@
         if with_column:
             column_copy(par, first, i).start()
 
-    def prepare(i, _):
+    def prepare(i, begin):
         slot = lax.rem(i, 2)
         land_copy(i, slot).wait()
 
         @pl.when(i + 1 < samples)
         def _():
-            land_copy(i + 1, 1 - slot).start()
+            land_start(i + 1, 1 - slot)
 
         def relayout(r, sums):
             new = []
@@ -126,10 +129,12 @@
 
         zero = jnp.zeros((8, LANES), F32)
         sums = lax.fori_loop(0, segrows, relayout, ((zero, zero), (zero, zero)))
+        if begin is None:
+            pl.semaphore_wait(barrier, devices - 1)
         send(0, True, i, sums, True)
         return 0
 
-    prepare(0, 0)
+    prepare(0, None)
     for copy in weight_copies:
         copy.start()
     zero_one = jnp.zeros((2 * LANES, LANES), BF16)
@@ -158,8 +163,6 @@
     came = lax.broadcasted_iota(jnp.int32, (px, px), 0)
     goes = lax.broadcasted_iota(jnp.int32, (px, px), 1)
     order[...] = jnp.where(goes == lax.rem(came, SEGS) * segrows + lax.div(came, SEGS), 1.0, 0.0).astype(BF16)
-    part[0, 0] = jnp.zeros((8, px), F32)
-    part[cols + 1, 2] = jnp.zeros((8, px), F32)
 
     lax.fori_loop(1, samples, prepare, 0)
     for copy in weight_copies:
@@ -230,16 +233,15 @@
             now, later = acts[s], acts[1 - s]
             if s == 0:
                 ahead = i + 1
-                await_copies(par, first, ahead, True)
+                await_copies(par, first, ahead, False)
             else:
                 ahead = jnp.minimum(i + 1, samples - 1)
 
                 @pl.when(i + 1 < samples)
                 def _():
-                    await_copies(par, first, ahead, True)
+                    await_copies(par, first, ahead, False)
 
             factors = norms(par, first, ahead, pair_of)
-            halo_column(par, first, ahead, later, factors)
 
             def quad(t, sums):
                 rows_of = []
@@ -290,6 +292,14 @@
                     column_copy(par, False, i + samples - DEFER).start()
 
             after(i)
+            if s == 0:
+                column_copy(par, first, ahead).wait()
+                halo_column(par, first, ahead, later, factors)
+            else:
+                @pl.when(i + 1 < samples)
+                def _():
+                    column_copy(par, first, ahead).wait()
+                    halo_column(par, first, ahead, later, factors)
 
         def two(t, _):
             step(2 * t, 0)
@@ -317,21 +327,26 @@
         await_copies(0, False, i, False)
         (scale, shift), = norms(0, False, i, rest_pair(5))
         buf = act_b.at[1]
-
+        prods = []
         for c in range(0, cols, 2):
             for e in range(2):
                 own_column(0, i, 0, c + e, buf.at[c + e + 1], scale, shift)
             both = jnp.concatenate([buf[c + e + 1].reshape(px + 2 * SEGS, LANES) for e in range(2)], axis=1)
-            prod = lax.dot_general(head_w[...], both, (((1,), (1,)), ((), ())), preferred_element_type=F32)
-            for e in range(2):
-                for kc in range(3):
-                    at = [72 * e + 24 * dr + 8 * kc for dr in range(3)]
-                    part[c + e + 1, kc] = sum(prod[at[dr]:at[dr] + 8, dr * SEGS:dr * SEGS + px] for dr in range(3))
-        q_send[i] = part[edge + 1, 2 * sx][0:4]
+            prods.append(lax.dot_general(head_w[...], both, (((1,), (1,)), ((), ())), preferred_element_type=F32))
+
+        def tap(c, dr, kc):
+            at = 72 * (c % 2) + 24 * dr + 8 * kc
+            return prods[c // 2][at:at + 8]
+
+        def shifted(taps):
+            return sum(taps[dr][:, dr * SEGS:dr * SEGS + px] for dr in range(3))
+
+        q_send[i] = shifted([jnp.where(sx == 0, tap(cols - 1, dr, 0), tap(0, dr, 2)) for dr in range(3)])[0:4]
         edge_copy(i).start()
         slot = lax.rem(i, 4)
         for c in range(cols):
-            y = part[c, 0] + part[c + 1, 1] + part[c + 2, 2]
+            near = [kc for kc in range(3) if 0 <= c + kc - 1 < cols]
+            y = shifted([sum(tap(c + kc - 1, dr, kc) for kc in near) for dr in range(3)])
             for ch in range(3):
                 image[slot, ch * cols + c:ch * cols + c + 1, :] = y[ch:ch + 1]
 
@@ -419,7 +434,6 @@
             pltpu.VMEM((144, 2 * LANES), F32),
             pltpu.VMEM((144, 2 * LANES), BF16),
             pltpu.VMEM((segrows * SEGS, segrows * SEGS), BF16),
-            pltpu.VMEM((cols + 2, 3, 8, segrows * SEGS), F32),
             pltpu.VMEM((4, 3 * cols, segrows * SEGS), F32),
             pltpu.VMEM((samples, 4, segrows * SEGS), F32),
             pltpu.VMEM((samples, 4, segrows * SEGS), F32),

time: 285 us -> 281 us (0.986)
  Pallas kernels: 282 us -> 278 us
    pallas_call x1, Pallas kernels: 282 us -> 278 us  [local_decode(): pl.pallas_call(functools.partial(decode_kernel, cfg), out_shape=jax.Shape...]
where the time goes in v4:
time: 281 us; the launch traced here: 280 us
  Pallas kernels  278 us (99%)
    pallas_call x1, Pallas kernels, local_decode(): pl.pallas_call(functools.partial(decode_kernel, cfg), out_shape=jax.Shape...  278 us

profile of v4, /device:TPU:0, one launch (start us, length us, event | category | flops | bytes accessed | tf_op | source)
XLA Modules:
  0.0 280.4 jit_solution(10990655012204957141)
XLA Ops:
  0.0 278.4 %shard_map.91 = f32[12,3,8,512]{3,2,1,0:T(8,128)} custom-call(bf16[12,16,32,8,256]{4,3,2,1,0:T(8,128)(2,1)} %bitcast.4, bf16[2,256]{1,0:T(2,128)(2,1)} %nf_ref.1, bf16[3,3,256,128]{3,2,1,0:T(8,128)(2,1)} %wf_hbm.1, bf16[256,128]{1,0:T(8,128)(2,1)} %ws_hbm.1, bf16[6,2,128]{2,1,0:T(2,128)(2,1)} %nr_ref.1, bf16[5,3,3,128,128]{4,3,2,1,0:T(8,128)(2,1)} %wr_hbm.1, ...), custom_call_target="tpu_custom_call" | custom-call | tf_op jit(solution)/shard_map/pallas_call | solution.py:450
  278.5 1.9 copy.11

commit v5 on v4

--- a/solution.py
+++ b/solution.py
@@ -9,7 +9,7 @@
 
 GROUPS = 32
 GN_EPS = 1e-6
-DEFER = 8
+DEFER = 9
 HEAD_LAG = 3
 EDGE_LAG = 5
 LANES = 128

time: 281 us -> 280 us (level)
  no operation moved by 1% of the time
where the time goes in v5:
time: 280 us; the launch traced here: 279 us
  Pallas kernels  277 us (99%)
    pallas_call x1, Pallas kernels, local_decode(): pl.pallas_call(functools.partial(decode_kernel, cfg), out_shape=jax.Shape...  277 us

profile of v5, /device:TPU:0, one launch (start us, length us, event | category | flops | bytes accessed | tf_op | source)
XLA Modules:
  0.0 279.2 jit_solution(7592698846240012017)
XLA Ops:
  0.0 277.2 %shard_map.91 = f32[12,3,8,512]{3,2,1,0:T(8,128)} custom-call(bf16[12,16,32,8,256]{4,3,2,1,0:T(8,128)(2,1)} %bitcast.4, bf16[2,256]{1,0:T(2,128)(2,1)} %nf_ref.1, bf16[3,3,256,128]{3,2,1,0:T(8,128)(2,1)} %wf_hbm.1, bf16[256,128]{1,0:T(8,128)(2,1)} %ws_hbm.1, bf16[6,2,128]{2,1,0:T(2,128)(2,1)} %nr_ref.1, bf16[5,3,3,128,128]{4,3,2,1,0:T(8,128)(2,1)} %wr_hbm.1, ...), custom_call_target="tpu_custom_call" | custom-call | tf_op jit(solution)/shard_map/pallas_call | solution.py:450
  277.3 1.9 copy.11
